TPU v7x, 32 devices: a whole 2x2x4 slice. The times are simulated.
32 devices in a mesh: pole: 4 (over y, core), dom: 8 (over z, x).
Axes of the slice: x: 2, y: 2, z: 4, core: 2. Of those that a mesh axis runs over, the one named last changes fastest.
Arguments:
- initial_block: bfloat16 [8, 8, 512, 256], P('dom'), may hold values from -24 to 24
- coupling: bfloat16 [8, 8, 512, 512], P('dom'), may hold values from -0.125 to 0.125
- pivots: bfloat16 [4, 8, 8, 2, 512, 512], P('pole', 'dom'), may hold values from -0.125 to 0.125
- interface: bfloat16 [4, 8, 3, 2, 512, 512], P('pole', 'dom'), may hold values from -0.1875 to 0.1875
- pole_values: float32 [4, 4], P('pole'), may hold values from 0.5 to 1.5
Outputs:
- filtered_basis: float32 [8, 8, 512, 256], P('dom', 'pole')
- rayleigh: float32 [256, 256], replicated
All inputs are finite; a program needn't handle non-finite values.
Results may differ from a plain program's by a relative error of at most 0.008.
Values sent between devices are 32-bit elements; how exact they have to be, the bound alone decides.
No kernel may reach another device: no remote copies, remote signals or barrier semaphores. Data moves between devices by JAX's collectives and lax.ppermute only.
A program may use at most 192 MiB of HBM per device.

v0:
```python
import jax
import jax.numpy as jnp
from jax import lax
from jax.sharding import PartitionSpec as P

B = 512
M = 256


def shifted(x, axis, by):
    length = lax.axis_size(axis)
    pairs = [(i, i + by) for i in range(length) if 0 <= i + by < length]
    return lax.ppermute(x, axis, pairs)


def lower_solve(factor, right_side):
    return lax.linalg.triangular_solve(factor, right_side, left_side=True, lower=True)


def complex_product(matrix, vectors):
    block_order = matrix.shape[1]
    half_width = vectors.shape[1] // 2
    stacked = matrix.reshape(2 * block_order, block_order)
    stacked_out = jnp.dot(stacked, vectors.astype(jnp.bfloat16), preferred_element_type=jnp.float32)
    real_part = stacked_out[:block_order, :half_width] - stacked_out[block_order:, half_width:]
    imag_part = stacked_out[:block_order, half_width:] + stacked_out[block_order:, :half_width]
    return jnp.concatenate([real_part, imag_part], axis=1)


def real_product(matrix, vectors):
    return jnp.dot(matrix, vectors.astype(jnp.bfloat16), preferred_element_type=jnp.float32)


def transposed_product(matrix, vectors):
    return lax.dot_general(
        matrix,
        vectors.astype(jnp.bfloat16),
        (((0,), (0,)), ((), ())),
        preferred_element_type=jnp.float32,
    )


def inner_products(left, right_side):
    return lax.dot_general(
        left,
        right_side,
        (((0,), (0,)), ((), ())),
        precision=lax.Precision.HIGHEST,
        preferred_element_type=jnp.float32,
    )


def partition_solve(inverse, coupled, source):
    previous = jnp.roll(coupled, 1, axis=0)
    initial = jnp.zeros(source.shape[1:], jnp.float32)

    def forward_step(carried, members):
        block_inverse, given, couple_prev = members
        result = complex_product(block_inverse, given + transposed_product(couple_prev, carried))
        return (result, result)

    unused, forward = lax.scan(forward_step, initial, (inverse, source, previous))

    def backward_step(carried, members):
        block_inverse, partial_value, couple_next = members
        result = partial_value + complex_product(block_inverse, real_product(couple_next, carried))
        return (result, result)

    unused, backward = lax.scan(backward_step, initial, (inverse, forward, coupled), reverse=True)
    return backward


def on_device(initial_block, coupling, pivots, interface, pole_values):
    blocks = coupling.shape[1]
    coupled = coupling[0]
    inverse = pivots[0, 0]
    factors = interface[0, 0]
    real_start = initial_block[0].astype(jnp.float32)
    source = jnp.concatenate([real_start, jnp.zeros_like(real_start)], axis=-1)
    first = partition_solve(inverse, coupled, source)
    bottom = first[blocks - 1]
    top = first[0]
    top_next = shifted(top, "dom", -1)
    below = complex_product(factors[0], bottom) - complex_product(factors[1], top_next)
    topmost = lax.axis_index("dom") == lax.axis_size("dom") - 1
    above = jnp.where(
        topmost, jnp.zeros_like(top_next), top_next - complex_product(factors[2], below)
    )
    link = coupled[blocks - 1]
    lifted = transposed_product(link, below)
    arriving = shifted(lifted, "dom", 1)
    update = source.at[0].add(arriving)
    update = update.at[blocks - 1].add(real_product(link, above))
    second = partition_solve(inverse, coupled, update)
    real_z = pole_values[0, 0]
    imag_z = pole_values[0, 1]
    real_w = pole_values[0, 2]
    imag_w = pole_values[0, 3]
    real_x = second[..., :M]
    imag_x = second[..., M:]
    filtered_term = real_w * real_x - imag_w * imag_x
    shifted_term = (
        (real_w * real_z - imag_w * imag_z) * real_x
        - (real_w * imag_z + imag_w * real_z) * imag_x
        - real_w * real_start
    )
    count = blocks // lax.axis_size("pole")
    summed = lax.psum(filtered_term, "pole")
    offset = lax.axis_index("pole") * count
    own_rows = lax.dynamic_slice_in_dim(summed, offset, count, 0).reshape(count * B, M)
    gram_part = inner_products(own_rows, own_rows)
    projected_part = inner_products(
        summed.reshape(blocks * B, M), shifted_term.reshape(blocks * B, M)
    )
    gram_total, projected_total = lax.psum((gram_part, projected_part), ("pole", "dom"))
    row_total = blocks * B * lax.axis_size("dom")
    gram = gram_total / row_total
    projected = projected_total / row_total
    factor = jnp.linalg.cholesky(gram)
    filtered_basis = lower_solve(factor, own_rows.T).T.reshape(1, count, B, M)
    middle = lower_solve(factor, projected)
    rayleigh = lower_solve(factor, middle.T).T
    return (filtered_basis, rayleigh)


def solution(mesh):
    in_specs = (
        P("dom", None, None, None),
        P("dom", None, None, None),
        P("pole", "dom", None, None, None, None),
        P("pole", "dom", None, None, None, None),
        P("pole", None),
    )
    out_specs = (P("dom", "pole", None, None), P())
    return jax.shard_map(
        on_device, mesh=mesh, in_specs=in_specs, out_specs=out_specs, check_vma=False
    )
```

profile of v0, /device:TPU:0, one launch (start us, length us, event | category | flops | bytes accessed | tf_op | source)
XLA Modules:
  0.0 687.2 jit_solution(11109018124211285651)
XLA Ops:
  7.2 4.2 slice_bitcast_fusion
  12.5 2.9 copy.17
  18.0 4.2 concatenate.76
  22.3 2.3 pad_maximum_fusion.2
  24.6 4.3 broadcast.158.clone.2
  29.7 65.2 %while.65 = (s32[]{:T(128)}, bf16[512,512]{0,1:T(8,128)(2,1)}, f32[8,512,512]{1,2,0:T(8,128)}, bf16[8,2,512,512]{3,2,1,0:T(8,128)(2,1)}, f32[8,512,512]{1,2,0:T(8,128)}, /*index=5*/bf16[8,512,512]{2,1,0:T(8,128)(2,1)}, s32[]{:T(128)}) while((s32[]{:T(128)}, bf16[512,512]{0,1:T(8,128)(2,1)}, f32[8,512,512]{1,2,0:T(8,128)}, ...), condition=%wide.region_1.2_spmd, body=%wide.region_0.1_spmd.sunk | while | flops 806617088 | bytes 17302612 | solution.py:62
  33.6 2.7 fusion.145
  41.8 2.7 fusion.145
  50.0 2.7 fusion.145
  58.1 2.7 fusion.145
  66.3 2.7 fusion.145
  74.5 2.7 fusion.145
  82.6 2.7 fusion.145
  90.7 2.7 fusion.145
  95.0 4.3 broadcast.158.clone.1
  99.3 67.7 %while.68 = (s32[]{:T(128)}, bf16[512,512]{0,1:T(8,128)(2,1)}, f32[8,512,512]{1,2,0:T(8,128)}, f32[8,512,512]{1,2,0:T(8,128)}, bf16[8,2,512,512]{3,2,1,0:T(8,128...) while((s32[]{:T(128)}, bf16[512,512]{0,1:T(8,128)(2,1)}, ...), condition=%wide.region_3.4_spmd.clone, body=%wide.region_2.3_spmd.clone.sunk | while | flops 807403520 | bytes 15204483 | solution.py:69
  103.0 2.5 fusion.154
  109.0 2.3 fusion.153
  111.5 2.4 fusion.154
  120.0 2.4 fusion.154
  128.5 2.4 fusion.154
  136.9 2.4 fusion.154
  142.9 2.3 fusion.153
  145.4 2.4 fusion.154
  153.9 2.4 fusion.154
  162.4 2.4 fusion.154
  173.8 22.5 %collective-permute-done = f32[512,512]{0,1:T(8,128)S(1)} collective-permute-done((f32[512,512]{0,1:T(8,128)S(1)}, f32[512,512]{0,1:T(8,128)S(1)}, u32[]{:S(2)}, u32[]{:S(2)}) %collective-permute-start) | collective-permute-done | bytes 1048608 | tf_op jit(solution)/shard_map/ppermute | solution.py:13
  197.6 2.5 convolution_bitcast_fusion.4
  200.0 6.1 collective-permute-start.1
  207.7 18.7 %collective-permute-done.1 = f32[512,512]{0,1:T(8,128)} collective-permute-done((f32[512,512]{0,1:T(8,128)}, f32[512,512]{0,1:T(8,128)}, u32[]{:S(2)}, u32[]{:S(2)}) %collective-permute-start.1) | collective-permute-done | bytes 1048608 | tf_op jit(solution)/shard_map/ppermute | solution.py:13
  226.4 2.3 fusion.65
  228.8 2.9 fusion.66
  231.7 4.3 broadcast.158.clone
  236.8 65.4 %while.66 = (s32[]{:T(128)}, bf16[512,512]{0,1:T(8,128)(2,1)}, f32[8,512,512]{1,2,0:T(8,128)}, bf16[8,2,512,512]{3,2,1,0:T(8,128)(2,1)}, f32[8,512,512]{1,2,0:T(8,128)}, /*index=5*/bf16[8,512,512]{2,1,0:T(8,128)(2,1)}, s32[]{:T(128)}) while((s32[]{:T(128)}, bf16[512,512]{0,1:T(8,128)(2,1)}, f32[8,512,512]{1,2,0:T(8,128)}, ...), condition=%wide.region_5.6_spmd, body=%wide.region_4.5_spmd.sunk | while | flops 806617088 | bytes 17302612 | solution.py:62
  240.7 2.7 fusion.149
  248.9 2.7 fusion.149
  257.0 2.7 fusion.149
  265.2 2.7 fusion.149
  273.4 2.7 fusion.149
  281.7 2.7 fusion.149
  289.9 2.7 fusion.149
  298.0 2.7 fusion.149
  302.3 4.3 broadcast.158
  306.6 67.7 %while.69 = (s32[]{:T(128)}, bf16[512,512]{0,1:T(8,128)(2,1)}, f32[8,512,512]{1,2,0:T(8,128)}, f32[8,512,512]{1,2,0:T(8,128)}, bf16[8,2,512,512]{3,2,1,0:T(8,128...) while((s32[]{:T(128)}, bf16[512,512]{0,1:T(8,128)(2,1)}, ...), condition=%wide.region_7.8_spmd.clone, body=%wide.region_6.7_spmd.clone.sunk | while | flops 807403520 | bytes 15204483 | solution.py:69
  310.3 2.5 fusion.158
  316.3 2.3 fusion.157
  318.8 2.4 fusion.158
  324.7 2.3 fusion.157
  327.3 2.4 fusion.158
  335.8 2.4 fusion.158
  344.2 2.4 fusion.158
  350.2 2.3 fusion.157
  352.7 2.4 fusion.158
  361.2 2.4 fusion.158
  369.6 2.4 fusion.158
  374.3 7.7 %multiply_subtract_fusion = f32[8,512,256]{1,2,0:T(8,128)} fusion(f32[8,512,512]{1,2,0:T(8,128)} %get-tuple-element.338, f32[]{:T(128)} %bitcast.27, f32[]{:T(128)} %bitcast.8), kind=kLoop, calls=%fused_computation.67 | loop fusion | flops 3145728 | bytes 12582920 | tf_op jit(solution)/shard_map/sub | solution.py:101
  387.1 81.9 %all-reduce.6.cloned.1.call-done = f32[8,512,256]{1,2,0:T(8,128)} async-done(((f32[8,512,256]{1,2,0:T(8,128)}), f32[8,512,256]{1,2,0:T(8,128)}) %all-reduce.6.cloned.1.call-update) | async-done | bytes 4194320 | tf_op jit(solution)/shard_map/psum | solution.py:108
  472.1 9.1 %fusion.61 = f32[256,256]{0,1:T(8,128)} fusion(f32[8,512,256]{1,2,0:T(8,128)S(1)} %copy-done.5, f32[8,512,512]{1,2,0:T(8,128)} %get-tuple-element.338, f32[]{:T(128)S(6)} %add.171, f32[]{:T(128)S(6)} %sub.71, f32[]{:T(128)} %bitcast.8, bf16[1,8,512,256]{2,3,1,0:T(8,128)(2,1)S(1)} %copy-done.3), kind=kOutput, calls=%fused_computation.82 | convolution fusion | flops 3227516928 | bytes 14942220 | tf_op jit(solution)/shard_map/dot_general | solution.py:44
  481.6 129.2 %all-reduce.8.cloned.1.call-done = (f32[256,256]{0,1:T(8,128)}, f32[256,256]{0,1:T(8,128)}) async-done(((f32[256,256]{0,1:T(8,128)}, f32[256,256]{0,1:T(8,128)}), (f32[256,256]{0,1:T(8,128)}, f32[256,256]{0,1:T(8,128)})) %all-reduce.8.cloned.1.call-update) | async-done | bytes 524304 | tf_op jit(solution)/shard_map/psum | solution.py:115
  613.1 11.7 %cholesky.50 = f32[128,128]{1,0:T(8,128)S(1)} custom-call(f32[128,128]{1,0:T(8,128)S(1)} %cholesky.118), custom_call_target="Cholesky" | custom-call | tf_op jit(solution)/shard_map/jit(cholesky)/cholesky | solution.py:119
  624.8 10.0 %custom-call.17 = f32[1,128,128]{1,2,0:T(8,128)S(1)} custom-call(f32[1,128,128]{2,1,0:T(8,128)S(1)} %get-tuple-element.517), custom_call_target="InvertDiagBlocksLowerTriangular" | custom-call | tf_op jit(solution)/shard_map/jit(cholesky)/cholesky | solution.py:119
  635.3 11.7 %cholesky.105 = f32[128,128]{1,0:T(8,128)S(1)} custom-call(f32[128,128]{1,0:T(8,128)S(1)} %convolution_subtract_fusion.3), custom_call_target="Cholesky" | custom-call | tf_op jit(solution)/shard_map/jit(cholesky)/cholesky | solution.py:119
  649.8 4.0 while.67
  653.7 19.7 %custom-call.18 = f32[2,128,128]{1,2,0:T(8,128)S(1)} custom-call(f32[2,128,128]{2,1,0:T(8,128)S(1)} %get-tuple-element.354), custom_call_target="InvertDiagBlocksLowerTriangular" | custom-call | tf_op jit(solution)/shard_map/triangular_solve | solution.py:17
  (212 shorter events, 205.6 us)
Async XLA Ops:
  7.2 461.8 %all-reduce.6.cloned.1.call-start = ((), (), s32[]{:S(2)}) async-start(), calls=%async_computation | async-start | bytes 8388608 | tf_op jit(solution)/shard_map/psum | solution.py:108
  15.4 6.9 %copy-start.2 = (bf16[1,8,512,256]{2,3,1,0:T(8,128)(2,1)}, bf16[1,8,512,256]{2,3,1,0:T(8,128)(2,1)S(1)}, u32[]{:S(2)}) copy-start(bf16[1,8,512,256]{2,3,1,0:T(8,128)(2,1)S(1)} %copy.17) | copy-start | bytes 6291460
  15.9 2.1 copy-start
  18.0 4.2 copy-start.4
  168.3 28.0 %collective-permute-start = (f32[512,512]{0,1:T(8,128)S(1)}, f32[512,512]{0,1:T(8,128)S(1)}, u32[]{:S(2)}, u32[]{:S(2)}) collective-permute-start(f32[512,512]{0,1:T(8,128)S(1)} %slice_bitcast_fusion.1), channel_id=1, source_target_pairs={{1,0},{2,1},{3,2},{4,3},{5,4},{6,5},{7,6},{9,8},{10,9},{11,10},{12... | collective-permute-start | bytes 3145736 | tf_op jit(solution)/shard_map/ppermute | solution.py:13
  197.1 9.1 %copy-start.6 = (f32[1,4]{1,0:T(1,128)S(1)}, f32[1,4]{1,0:T(1,128)}, u32[]{:S(2)}) copy-start(f32[1,4]{1,0:T(1,128)} %param.23) | copy-start | bytes 52
  200.0 26.4 %collective-permute-start.1 = (f32[512,512]{0,1:T(8,128)}, f32[512,512]{0,1:T(8,128)}, u32[]{:S(2)}, u32[]{:S(2)}) collective-permute-start(f32[512,512]{0,1:T(8,128)} %convolution_bitcast_fusion.4), channel_id=1, source_target_pairs={{0,1},{1,2},{2,3},{3,4},{4,5},{5,6},{6,7},{8,9},{9,10},{10,11},{11... | collective-permute-start | bytes 3145736 | tf_op jit(solution)/shard_map/ppermute | solution.py:13
  206.1 20.3 %copy-start.1 = (f32[8,512,256]{1,2,0:T(8,128)S(1)}, f32[8,512,256]{1,2,0:T(8,128)}, u32[]{:S(2)}) copy-start(f32[8,512,256]{1,2,0:T(8,128)} %copy-done) | copy-start | bytes 12582916
  382.0 90.2 %copy-start.3 = (bf16[1,8,512,256]{2,3,1,0:T(8,128)(2,1)S(1)}, bf16[1,8,512,256]{2,3,1,0:T(8,128)(2,1)}, u32[]{:S(2)}) copy-start(bf16[1,8,512,256]{2,3,1,0:T(8,128)(2,1)} %copy-done.2) | copy-start | bytes 6291460
  382.0 228.9 %all-reduce.8.cloned.1.call-start = ((), (), s32[]{:S(2)}) async-start(), calls=%async_computation.1 | async-start | bytes 1048576 | tf_op jit(solution)/shard_map/psum | solution.py:115
  469.0 3.2 copy-start.5
Sparse Core Ops, SparseCore 0:
  382.1 86.7 all-reduce.5
  481.4 129.4 all-reduce.7
where the time goes:
time: 699 us; the launch traced here: 687 us
  waiting for transfers between devices  252 us (36%)
  other arithmetic  173 us (25%)
  local copies, waits for them, and re-layouts  128 us (18%)
  matrix products  104 us (15%)
  between operations  20.8 us (3%)
  starting transfers between devices  7.59 us (1%)
    psum x1, waiting for transfers between devices, on_device(): lax.psum((gram_part, projected_part), ('pole', 'dom'))  129 us
    dot_general x35, matrix products, complex_product(): jnp.dot(stacked, vectors.astype(jnp.bfloat16), preferred_element_type=jnp...  83.1 us
    dynamic_slice x64, local copies, waits for them, and re-layouts, partition_solve(): lax.scan(forward_step, initial, (inverse, source, previous))  82.9 us
    psum x1, waiting for transfers between devices, on_device(): summed = lax.psum(filtered_term, 'pole')  81.9 us
    dynamic_update_slice x32, other arithmetic, partition_solve(): lax.scan(forward_step, initial, (inverse, source, previous))  60.9 us
    ppermute x2, waiting for transfers between devices, shifted(): return lax.ppermute(x, axis, pairs)  41.1 us
    add x16, other arithmetic, backward_step(): partial_value + complex_product(block_inverse, real_product(couple_next,...  35.2 us
    another operation x7, other arithmetic, on_device(): factor = jnp.linalg.cholesky(gram)  34.8 us
  transfers between devices with their start and end apart: 4, of which 4 were waited for; matrix products, arithmetic and copies ran while one was open for 1% of the time, Pallas kernels for 0%

commit v1 on v0

--- a/solution.py
+++ b/solution.py
@@ -105,7 +105,7 @@
         - real_w * real_start
     )
     count = blocks // lax.axis_size("pole")
-    summed = lax.psum(filtered_term, "pole")
+    summed = jnp.sum(lax.all_gather(filtered_term, "pole"), axis=0)
     offset = lax.axis_index("pole") * count
     own_rows = lax.dynamic_slice_in_dim(summed, offset, count, 0).reshape(count * B, M)
     gram_part = inner_products(own_rows, own_rows)

time: 699 us -> 735 us (1.052)
  waiting for transfers between devices: 252 us -> 273 us
  other arithmetic: 173 us -> 183 us
    all_gather x0 -> x1, waiting for transfers between devices: none -> 102 us  [on_device(): summed = jnp.sum(lax.all_gather(filtered_term, 'pole'), axis=0)]
    psum x1 -> x0, waiting for transfers between devices: 81.9 us -> none  [on_device(): summed = lax.psum(filtered_term, 'pole')]
    unnamed x3 -> x4, other arithmetic: 0.01 us -> 9.72 us
where the time goes in v1:
time: 735 us; the launch traced here: 724 us
  waiting for transfers between devices  273 us (37%)
  other arithmetic  183 us (25%)
  local copies, waits for them, and re-layouts  133 us (18%)
  matrix products  105 us (14%)
  between operations  20.7 us (3%)
  starting transfers between devices  7.77 us (1%)
    psum x1, waiting for transfers between devices, on_device(): lax.psum((gram_part, projected_part), ('pole', 'dom'))  129 us
    all_gather x1, waiting for transfers between devices, on_device(): summed = jnp.sum(lax.all_gather(filtered_term, 'pole'), axis=0)  102 us
    dot_general x35, matrix products, complex_product(): jnp.dot(stacked, vectors.astype(jnp.bfloat16), preferred_element_type=jnp...  83.1 us
    dynamic_slice x64, local copies, waits for them, and re-layouts, partition_solve(): lax.scan(forward_step, initial, (inverse, source, previous))  82.9 us
    dynamic_update_slice x32, other arithmetic, partition_solve(): lax.scan(forward_step, initial, (inverse, source, previous))  60.9 us
    ppermute x2, waiting for transfers between devices, shifted(): return lax.ppermute(x, axis, pairs)  41.3 us
    add x16, other arithmetic, backward_step(): partial_value + complex_product(block_inverse, real_product(couple_next,...  35.3 us
    another operation x7, other arithmetic, on_device(): factor = jnp.linalg.cholesky(gram)  34.7 us
  transfers between devices with their start and end apart: 4, of which 4 were waited for; matrix products, arithmetic and copies ran while one was open for 1% of the time, Pallas kernels for 0%

profile of v1, /device:TPU:0, one launch (start us, length us, event | category | flops | bytes accessed | tf_op | source)
XLA Modules:
  0.0 723.7 jit_solution(5081764581090901401)
XLA Ops:
  7.2 4.2 slice_bitcast_fusion
  12.5 2.9 copy.18
  18.0 4.2 concatenate.76
  22.3 2.3 pad_maximum_fusion.2
  24.6 4.3 broadcast.158.clone.2
  29.7 65.2 %while.65 = (s32[]{:T(128)}, bf16[512,512]{0,1:T(8,128)(2,1)}, f32[8,512,512]{1,2,0:T(8,128)}, bf16[8,2,512,512]{3,2,1,0:T(8,128)(2,1)}, f32[8,512,512]{1,2,0:T(8,128)}, /*index=5*/bf16[8,512,512]{2,1,0:T(8,128)(2,1)}, s32[]{:T(128)}) while((s32[]{:T(128)}, bf16[512,512]{0,1:T(8,128)(2,1)}, f32[8,512,512]{1,2,0:T(8,128)}, ...), condition=%wide.region_1.2_spmd, body=%wide.region_0.1_spmd.sunk | while | flops 806617088 | bytes 17302612 | solution.py:62
  33.6 2.7 fusion.145
  41.8 2.7 fusion.145
  50.0 2.7 fusion.145
  58.1 2.7 fusion.145
  66.3 2.7 fusion.145
  74.5 2.7 fusion.145
  82.6 2.7 fusion.145
  90.7 2.7 fusion.145
  95.0 4.3 broadcast.158.clone.1
  99.3 67.7 %while.68 = (s32[]{:T(128)}, bf16[512,512]{0,1:T(8,128)(2,1)}, f32[8,512,512]{1,2,0:T(8,128)}, f32[8,512,512]{1,2,0:T(8,128)}, bf16[8,2,512,512]{3,2,1,0:T(8,128...) while((s32[]{:T(128)}, bf16[512,512]{0,1:T(8,128)(2,1)}, ...), condition=%wide.region_3.4_spmd.clone, body=%wide.region_2.3_spmd.clone.sunk | while | flops 807403520 | bytes 15204483 | solution.py:69
  103.0 2.5 fusion.154
  111.5 2.4 fusion.154
  120.0 2.4 fusion.154
  128.5 2.4 fusion.154
  136.9 2.4 fusion.154
  145.4 2.4 fusion.154
  153.9 2.4 fusion.154
  162.4 2.4 fusion.154
  173.8 22.5 %collective-permute-done = f32[512,512]{0,1:T(8,128)S(1)} collective-permute-done((f32[512,512]{0,1:T(8,128)S(1)}, f32[512,512]{0,1:T(8,128)S(1)}, u32[]{:S(2)}, u32[]{:S(2)}) %collective-permute-start) | collective-permute-done | bytes 1048608 | tf_op jit(solution)/shard_map/ppermute | solution.py:13
  197.6 2.5 convolution_bitcast_fusion.4
  200.0 5.9 collective-permute-start.1
  207.6 18.9 %collective-permute-done.1 = f32[512,512]{0,1:T(8,128)} collective-permute-done((f32[512,512]{0,1:T(8,128)}, f32[512,512]{0,1:T(8,128)}, u32[]{:S(2)}, u32[]{:S(2)}) %collective-permute-start.1) | collective-permute-done | bytes 1048608 | tf_op jit(solution)/shard_map/ppermute | solution.py:13
  226.4 2.3 fusion.65
  228.8 2.9 fusion.66
  231.7 4.3 broadcast.158.clone
  236.8 65.4 %while.66 = (s32[]{:T(128)}, bf16[512,512]{0,1:T(8,128)(2,1)}, f32[8,512,512]{1,2,0:T(8,128)}, bf16[8,2,512,512]{3,2,1,0:T(8,128)(2,1)}, f32[8,512,512]{1,2,0:T(8,128)}, /*index=5*/bf16[8,512,512]{2,1,0:T(8,128)(2,1)}, s32[]{:T(128)}) while((s32[]{:T(128)}, bf16[512,512]{0,1:T(8,128)(2,1)}, f32[8,512,512]{1,2,0:T(8,128)}, ...), condition=%wide.region_5.6_spmd, body=%wide.region_4.5_spmd.sunk | while | flops 806617088 | bytes 17302612 | solution.py:62
  240.7 2.7 fusion.149
  248.9 2.7 fusion.149
  257.0 2.7 fusion.149
  265.2 2.7 fusion.149
  273.4 2.7 fusion.149
  281.7 2.7 fusion.149
  289.9 2.7 fusion.149
  298.0 2.7 fusion.149
  302.3 4.3 broadcast.158
  306.6 67.8 %while.69 = (s32[]{:T(128)}, bf16[512,512]{0,1:T(8,128)(2,1)}, f32[8,512,512]{1,2,0:T(8,128)}, f32[8,512,512]{1,2,0:T(8,128)}, bf16[8,2,512,512]{3,2,1,0:T(8,128...) while((s32[]{:T(128)}, bf16[512,512]{0,1:T(8,128)(2,1)}, ...), condition=%wide.region_7.8_spmd.clone, body=%wide.region_6.7_spmd.clone.sunk | while | flops 807403520 | bytes 15204483 | solution.py:69
  310.3 2.5 fusion.158
  316.3 2.3 fusion.157
  318.8 2.4 fusion.158
  327.3 2.4 fusion.158
  333.3 2.3 fusion.157
  335.8 2.4 fusion.158
  344.3 2.4 fusion.158
  352.8 2.4 fusion.158
  361.3 2.4 fusion.158
  369.7 2.4 fusion.158
  374.4 7.6 %multiply_subtract_fusion = f32[8,512,256]{1,2,0:T(8,128)} fusion(f32[8,512,512]{1,2,0:T(8,128)} %get-tuple-element.338, f32[]{:T(128)} %bitcast.27, f32[]{:T(128)} %bitcast.8), kind=kLoop, calls=%fused_computation.67 | loop fusion | flops 3145728 | bytes 12582920 | tf_op jit(solution)/shard_map/sub | solution.py:101
  382.0 5.4 copy.21
  392.8 102.0 %all-gather.3.cloned.1.call-done = f32[32,512,256]{2,1,0:T(8,128)} async-done(((f32[8,512,256]{2,1,0:T(8,128)}), f32[32,512,256]{2,1,0:T(8,128)}) %all-gather.3.cloned.1.call-update) | async-done | bytes 16777232 | tf_op jit(solution)/shard_map/all_gather | solution.py:108
  494.8 9.7 %reduce_sum.9 = f32[8,512,256]{2,1,0:T(8,128)} reduce(f32[4,8,512,256]{3,2,1,0:T(8,128)} %bitcast.224, f32[]{:T(128)} %constant.243.clone.1), dimensions={0}, to_apply=%region_8.9 | reduce | flops 3145728 | bytes 20971524
  506.0 2.5 convolution_bitcast_fusion.5
  508.5 9.3 %fusion.61 = f32[256,256]{0,1:T(8,128)} fusion(f32[8,512,256]{2,1,0:T(8,128)S(1)} %copy-done.2, f32[8,512,512]{1,2,0:T(8,128)} %get-tuple-element.338, f32[]{:T(128)S(6)} %add.169, f32[]{:T(128)S(6)} %sub.71, f32[]{:T(128)} %bitcast.8, bf16[1,8,512,256]{2,3,1,0:T(8,128)(2,1)S(1)} %copy-done.4), kind=kOutput, calls=%fused_computation.82 | convolution fusion | flops 3227516928 | bytes 14942220 | tf_op jit(solution)/shard_map/dot_general | solution.py:44
  517.8 129.5 %all-reduce.5.cloned.1.call-done = (f32[256,256]{0,1:T(8,128)}, f32[256,256]{0,1:T(8,128)}) async-done(((f32[256,256]{0,1:T(8,128)}, f32[256,256]{0,1:T(8,128)}), (f32[256,256]{0,1:T(8,128)}, f32[256,256]{0,1:T(8,128)})) %all-reduce.5.cloned.1.call-update) | async-done | bytes 524304 | tf_op jit(solution)/shard_map/psum | solution.py:115
  649.4 11.9 %cholesky.50 = f32[128,128]{1,0:T(8,128)S(1)} custom-call(f32[128,128]{1,0:T(8,128)S(1)} %cholesky.118), custom_call_target="Cholesky" | custom-call | tf_op jit(solution)/shard_map/jit(cholesky)/cholesky | solution.py:119
  661.4 9.8 %custom-call.17 = f32[1,128,128]{1,2,0:T(8,128)S(1)} custom-call(f32[1,128,128]{2,1,0:T(8,128)S(1)} %get-tuple-element.517), custom_call_target="InvertDiagBlocksLowerTriangular" | custom-call | tf_op jit(solution)/shard_map/jit(cholesky)/cholesky | solution.py:119
  671.7 11.7 %cholesky.105 = f32[128,128]{1,0:T(8,128)S(1)} custom-call(f32[128,128]{1,0:T(8,128)S(1)} %convolution_subtract_fusion.3), custom_call_target="Cholesky" | custom-call | tf_op jit(solution)/shard_map/jit(cholesky)/cholesky | solution.py:119
  686.1 4.2 while.67
  690.3 19.7 %custom-call.18 = f32[2,128,128]{1,2,0:T(8,128)S(1)} custom-call(f32[2,128,128]{2,1,0:T(8,128)S(1)} %get-tuple-element.354), custom_call_target="InvertDiagBlocksLowerTriangular" | custom-call | tf_op jit(solution)/shard_map/triangular_solve | solution.py:17
  (213 shorter events, 210.9 us)
Async XLA Ops:
  7.2 487.6 %all-gather.3.cloned.1.call-start = ((), (), s32[]{:S(2)}) async-start(), calls=%async_computation | async-start | bytes 20971520 | tf_op jit(solution)/shard_map/all_gather | solution.py:108
  15.4 6.9 copy-start.3
  15.9 2.1 copy-start
  18.0 4.2 copy-start.5
  168.3 28.0 %collective-permute-start = (f32[512,512]{0,1:T(8,128)S(1)}, f32[512,512]{0,1:T(8,128)S(1)}, u32[]{:S(2)}, u32[]{:S(2)}) collective-permute-start(f32[512,512]{0,1:T(8,128)S(1)} %slice_bitcast_fusion.1), channel_id=1, source_target_pairs={{1,0},{2,1},{3,2},{4,3},{5,4},{6,5},{7,6},{9,8},{10,9},{11,10},{12... | collective-permute-start | bytes 3145736 | tf_op jit(solution)/shard_map/ppermute | solution.py:13
  197.1 8.9 %copy-start.6 = (f32[1,4]{1,0:T(1,128)S(1)}, f32[1,4]{1,0:T(1,128)}, u32[]{:S(2)}) copy-start(f32[1,4]{1,0:T(1,128)} %param.23) | copy-start | bytes 52
  200.0 26.4 %collective-permute-start.1 = (f32[512,512]{0,1:T(8,128)}, f32[512,512]{0,1:T(8,128)}, u32[]{:S(2)}, u32[]{:S(2)}) collective-permute-start(f32[512,512]{0,1:T(8,128)} %convolution_bitcast_fusion.4), channel_id=1, source_target_pairs={{0,1},{1,2},{2,3},{3,4},{4,5},{5,6},{6,7},{8,9},{9,10},{10,11},{11... | collective-permute-start | bytes 3145736 | tf_op jit(solution)/shard_map/ppermute | solution.py:13
  206.0 20.5 %copy-start.1 = (f32[8,512,256]{1,2,0:T(8,128)S(1)}, f32[8,512,256]{1,2,0:T(8,128)}, u32[]{:S(2)}) copy-start(f32[8,512,256]{1,2,0:T(8,128)} %copy-done) | copy-start | bytes 12582916
  387.4 259.8 %all-reduce.5.cloned.1.call-start = ((), (), s32[]{:S(2)}) async-start(), calls=%async_computation.1 | async-start | bytes 1048576 | tf_op jit(solution)/shard_map/psum | solution.py:115
  494.8 13.7 %copy-start.4 = (bf16[1,8,512,256]{2,3,1,0:T(8,128)(2,1)S(1)}, bf16[1,8,512,256]{2,3,1,0:T(8,128)(2,1)}, u32[]{:S(2)}) copy-start(bf16[1,8,512,256]{2,3,1,0:T(8,128)(2,1)} %copy-done.3) | copy-start | bytes 6291460
  504.5 4.0 copy-start.2
Sparse Core Ops, SparseCore 0:
  387.5 107.2 all-gather.2
  517.9 129.3 all-reduce.4
